TPU v7x, 32 devices: a whole 2x2x4 slice. The times are simulated.
32 devices in a mesh: lat: 8 (over z, y), chan: 4 (over x, core).
Axes of the slice: x: 2, y: 2, z: 4, core: 2. Of those that a mesh axis runs over, the one named last changes fastest.
Arguments:
- grid_in: bfloat16 [256, 384, 1024], P('chan', 'lat'), may hold values from -6 to 6
- quad_weights: float32 [384], P('lat'), may hold values from 0.5 to 2
- legendre: bfloat16 [384, 384, 384], P('lat'), as said below
- mixing: bfloat16 [2, 384, 256, 256], P(None, 'lat', 'chan'), may hold values from -0.375 to 0.375
Outputs:
- grid_out: bfloat16 [256, 384, 1024], P('chan', 'lat')
Inputs may be any that keep to these rules, and one draw needn't show every extreme that they name: legendre[m, l, t] is zero wherever l < m.
All inputs are finite; a program needn't handle non-finite values.
Results may differ from a plain program's by a relative error of at most 0.0068.
Values may be sent and summed in bfloat16 or wider, within the bound.
A program may use at most 128 MiB of HBM per device.

v0:
```python
import math

import jax
import jax.numpy as jnp
from jax import lax
from jax.sharding import PartitionSpec as P

M = 384


def fourier_table(number, length):
    orders = jnp.arange(number, dtype=jnp.int32)
    points = jnp.arange(length, dtype=jnp.int32)
    phases = orders[:, None] * points[None, :] % length
    angles = phases.astype(jnp.float32) * (2.0 * math.pi / length)
    factor = 1.0 / math.sqrt(length)
    return jnp.stack([jnp.cos(angles) * factor, -jnp.sin(angles) * factor]).astype(jnp.bfloat16)


def body(grid_in, quad_weights, legendre, mixing):
    groups = grid_in.shape[0]
    rows_lat = grid_in.shape[1]
    length = grid_in.shape[2]
    fourier = fourier_table(M, length)
    spectra = jnp.einsum("ctn,rmn->mtrc", grid_in, fourier, preferred_element_type=jnp.float32)
    spectra = spectra * quad_weights[None, :, None, None]
    weighted = spectra.astype(jnp.bfloat16).reshape(M, rows_lat, 2 * groups)
    coeffs = jnp.einsum(
        "mlt,mtk->mlk",
        legendre,
        lax.all_to_all(weighted, "lat", split_axis=0, concat_axis=1, tiled=True),
        preferred_element_type=jnp.float32,
    ).astype(jnp.bfloat16)
    by_degree = lax.all_to_all(coeffs, "lat", split_axis=1, concat_axis=0, tiled=True)
    orders = by_degree.shape[0]
    degrees = by_degree.shape[1]
    weights_out = lax.all_to_all(mixing, "chan", split_axis=3, concat_axis=2, tiled=True)
    block_in = lax.all_gather(by_degree, "chan", axis=2, tiled=True)
    shards = block_in.shape[2] // (2 * groups)
    halves = block_in.reshape(orders, degrees, shards, 2, groups)
    real_in = halves[:, :, :, 0, :].reshape(orders, degrees, shards * groups)
    imag_in = halves[:, :, :, 1, :].reshape(orders, degrees, shards * groups)
    real_weight = weights_out[0]
    imag_weight = weights_out[1]
    real_sum = jnp.einsum(
        "mlc,lcd->mld", real_in, real_weight, preferred_element_type=jnp.float32
    ) - jnp.einsum("mlc,lcd->mld", imag_in, imag_weight, preferred_element_type=jnp.float32)
    imag_sum = jnp.einsum(
        "mlc,lcd->mld", imag_in, real_weight, preferred_element_type=jnp.float32
    ) + jnp.einsum("mlc,lcd->mld", real_in, imag_weight, preferred_element_type=jnp.float32)
    mixed_coef = (
        jnp.stack([real_sum, imag_sum], axis=2)
        .reshape(orders, degrees, 2 * groups)
        .astype(jnp.bfloat16)
    )
    synthesis = jnp.einsum(
        "mlt,mlk->mtk",
        legendre,
        lax.all_to_all(mixed_coef, "lat", split_axis=0, concat_axis=1, tiled=True),
        preferred_element_type=jnp.float32,
    ).astype(jnp.bfloat16)
    gridded = lax.all_to_all(synthesis, "lat", split_axis=1, concat_axis=0, tiled=True)
    spread = gridded.reshape(M, rows_lat, 2, groups)
    restored = jnp.einsum("mtrc,rmn->ctn", spread, fourier, preferred_element_type=jnp.float32)
    return (restored + grid_in.astype(jnp.float32)).astype(jnp.bfloat16)


def solution(mesh):
    return jax.shard_map(
        body,
        mesh=mesh,
        in_specs=(
            P("chan", "lat", None),
            P("lat"),
            P("lat", None, None),
            P(None, "lat", "chan", None),
        ),
        out_specs=P("chan", "lat", None),
        check_vma=False,
    )
```

profile of v0, /device:TPU:0, one launch (start us, length us, event | category | flops | bytes accessed | tf_op | source)
XLA Modules:
  0.0 787.6 jit_solution(417036485185853445)
XLA Ops:
  6.5 0.0 all-gather.2.cloned.1.call-start
  6.5 6.4 multiply_convert_fusion.1
  13.0 0.0 copy-start.4
  13.0 0.0 copy-start.6
  13.0 0.9 copy-done.4
  13.9 0.3 copy-done.6
  14.1 15.9 %fusion.4 = bf16[384,48,2,64]{0,3,1,2:T(8,128)(2,1)S(1)} fusion(f32[48]{0:T(128)} %param.5, bf16[64,48,1024]{2,1,0:T(8,128)(2,1)} %param.4, bf16[1,384,1024]{2,1,0:T(8,128)(2,1)S(1)} %get-tuple-element.9, bf16[1,384,1024]{2,1,0:T(8,128)(2,1)S(1)} %get-tuple-element.10), kind=kOutput, calls=%fused_computation.7 | convolution fusion | flops 4839702528 | bytes 12583104 | tf_op jit(solution)/shard_map/ctn,rmn->mtrc/dot_general | solution.py:25
  30.0 2.7 copy.33
  32.8 7.0 copy.34
  39.7 112.2 %all_to_all.84 = bf16[384,48,128]{2,1,0:T(8,128)(2,1)S(1)} all-to-all(bf16[384,48,128]{2,1,0:T(8,128)(2,1)} %copy.34), channel_id=1, replica_groups=mesh['lat'=8,'chan'=4] {'lat'}, dimensions={0} | all-to-all | bytes 9437184 | tf_op jit(solution)/shard_map/all_to_all | solution.py:31
  151.9 1.4 copy.35
  153.3 9.2 %convert_bitcast_fusion.1 = bf16[48,384,128]{1,2,0:T(8,128)(2,1)} fusion(bf16[48,384,128]{2,1,0:T(8,128)(2,1)S(1)} %bitcast.87, bf16[48,384,384]{2,1,0:T(8,128)(2,1)} %param.6), kind=kOutput, calls=%fused_computation.12 | convolution fusion | flops 1814298624 | bytes 23592960 | tf_op jit(solution)/shard_map/mlt,mtk->mlk/dot_general | solution.py:28
  162.4 7.0 copy.37
  169.4 107.9 %all_to_all.85 = bf16[48,384,128]{2,0,1:T(8,128)(2,1)S(1)} all-to-all(bf16[48,384,128]{2,0,1:T(8,128)(2,1)} %copy.37), channel_id=1, replica_groups=mesh['lat'=8,'chan'=4] {'lat'}, dimensions={1} | all-to-all | bytes 9437184 | tf_op jit(solution)/shard_map/all_to_all | solution.py:34
  277.3 3.4 copy.39
  280.7 0.0 copy-start.3
  280.7 0.0 all-gather.2.cloned.1.call-update
  280.7 1.9 copy-done.3
  282.6 9.4 %copy.41 = bf16[2,48,64,256]{2,1,0,3:T(8,128)(2,1)} copy(bf16[2,48,64,256]{3,2,1,0:T(8,128)(2,1)S(1)} %copy-done.3) | data formatting | bytes 6291456 | tf_op args[3]
  292.0 7.2 reshape.101
  299.2 74.5 %all_to_all.86 = bf16[4,2,196608]{2,1,0:T(2,128)(2,1)} all-to-all(bf16[4,2,196608]{2,1,0:T(2,128)(2,1)S(1)} %reshape.101), channel_id=1, replica_groups=mesh['lat'=8,'chan'=4] {'chan'}, dimensions={0} | all-to-all | bytes 6291456 | tf_op jit(solution)/shard_map/all_to_all | solution.py:37
  373.8 7.5 reshape.102
  381.3 8.2 %copy.77 = bf16[2,48,64,4,64]{2,3,4,1,0:T(4,128)(2,1)S(1)} copy(bf16[2,48,64,4,64]{2,1,0,4,3:T(8,128)(2,1)} %bitcast.89) | data formatting | bytes 6291456 | tf_op jit(solution)/shard_map/all_to_all | solution.py:37
  389.5 4.3 fusion.20
  393.8 0.0 copy-start.1
  393.8 5.9 squeeze.7
  399.7 0.0 copy-done.1
  399.7 2.9 squeeze.6
  402.6 33.2 %all-gather.2.cloned.1.call-done = bf16[384,48,512]{2,1,0:T(8,128)(2,1)} async-done(((bf16[384,48,128]{2,1,0:T(8,128)(2,1)}), bf16[384,48,512]{2,1,0:T(8,128)(2,1)}) %all-gather.2.cloned.1.call-update) | async-done | bytes 18874384 | tf_op jit(solution)/shard_map/all_gather | solution.py:38
  435.9 25.8 %copy.40 = bf16[384,48,512]{0,2,1:T(8,128)(2,1)} copy(bf16[384,48,512]{2,1,0:T(8,128)(2,1)} %all-gather.2.cloned.1.call-done) | data formatting | bytes 37748736 | tf_op jit(solution)/shard_map/all_gather | solution.py:38
  461.6 0.0 copy-start
  461.6 8.4 %fusion.19 = (bf16[384,48,4,1,64]{0,4,3,2,1:T(8,128)(2,1)S(1)}, bf16[384,48,4,1,64]{0,4,3,2,1:T(8,128)(2,1)S(1)}) fusion(bf16[384,48,4,2,64]{0,4,3,2,1:T(8,128)(2,1)} %bitcast.85), kind=kLoop, calls=%fused_computation.31 | loop fusion | bytes 37748736 | tf_op jit(solution)/shard_map/slice | solution.py:41
  470.0 0.0 copy-done
  470.0 1.5 fusion.21
  471.6 1.5 fusion.22
  473.1 4.7 fusion.7
  477.8 0.0 copy-start.2
  477.8 3.4 fusion.8
  481.2 0.0 copy-done.2
  481.2 0.5 pad_maximum_fusion
  481.7 2.7 copy.47
  484.5 7.0 copy.48
  491.4 110.3 %all_to_all.87 = bf16[384,48,128]{2,1,0:T(8,128)(2,1)S(1)} all-to-all(bf16[384,48,128]{2,1,0:T(8,128)(2,1)} %copy.48), channel_id=1, replica_groups=mesh['lat'=8,'chan'=4] {'lat'}, dimensions={0} | all-to-all | bytes 9437184 | tf_op jit(solution)/shard_map/all_to_all | solution.py:59
  601.7 1.4 copy.49
  603.1 10.5 %convert_bitcast_fusion = bf16[48,384,128]{1,2,0:T(8,128)(2,1)} fusion(bf16[48,384,128]{2,1,0:T(8,128)(2,1)S(1)} %bitcast.86, bf16[48,384,384]{2,1,0:T(8,128)(2,1)} %param.6), kind=kOutput, calls=%fused_computation.9 | convolution fusion | flops 1814298624 | bytes 23592960 | tf_op jit(solution)/shard_map/mlt,mlk->mtk/dot_general | solution.py:56
  613.6 7.0 copy.51
  620.6 108.7 %all_to_all.88 = bf16[48,384,128]{2,0,1:T(8,128)(2,1)} all-to-all(bf16[48,384,128]{2,0,1:T(8,128)(2,1)} %copy.51), channel_id=1, replica_groups=mesh['lat'=8,'chan'=4] {'lat'}, dimensions={1} | all-to-all | bytes 9437184 | tf_op jit(solution)/shard_map/all_to_all | solution.py:62
  729.3 12.4 %copy.67 = bf16[8,48,48,128]{1,0,3,2:T(8,128)(2,1)} copy(bf16[8,48,48,128]{3,1,2,0:T(8,128)(2,1)} %bitcast.97) | data formatting | bytes 9437184 | tf_op jit(solution)/shard_map/reshape | solution.py:63
  741.6 0.0 copy-start.5
  741.6 0.0 copy-start.7
  741.6 16.9 %reshape.100 = bf16[384,48,2,64]{0,3,2,1:T(8,128)(2,1)} reshape(bf16[8,48,48,128]{1,0,3,2:T(8,128)(2,1)} %copy.67) | data formatting | bytes 9437184 | tf_op jit(solution)/shard_map/reshape | solution.py:63
  758.6 0.0 copy-done.5
  758.6 0.0 copy-done.7
  758.6 15.5 %fusion = bf16[64,48,1024]{2,0,1:T(8,128)(2,1)S(1)} fusion(bf16[64,48,1024]{2,1,0:T(8,128)(2,1)} %param.4, bf16[384,48,2,64]{0,3,2,1:T(8,128)(2,1)} %reshape.100, bf16[1,384,1024]{2,1,0:T(8,128)(2,1)S(1)} %copy-done.5, bf16[1,384,1024]{2,1,0:T(8,128)(2,1)S(1)} %copy-done.7), kind=kOutput, calls=%fused_computation.1 | convolution fusion | flops 4844421120 | bytes 18874368 | tf_op jit(solution)/shard_map/mtrc,rmn->ctn/dot_general | solution.py:64
  774.1 6.2 copy.56
Async XLA Ops:
  6.5 429.3 %all-gather.2.cloned.1.call-start = ((), (), s32[]{:S(2)}) async-start(), calls=%async_computation.5 | async-start | bytes 23592960 | tf_op jit(solution)/shard_map/all_gather | solution.py:38
  13.0 0.9 copy-start.4
  13.0 1.1 copy-start.6
  280.7 1.9 copy-start.3
  393.8 5.9 copy-start.1
  461.6 8.4 %copy-start = (bf16[48,256,64]{1,2,0:T(8,128)(2,1)S(1)}, bf16[48,256,64]{1,2,0:T(8,128)(2,1)}, u32[]{:S(2)}) copy-start(bf16[48,256,64]{1,2,0:T(8,128)(2,1)} %squeeze.6) | copy-start | bytes 4718596
  477.8 3.4 copy-start.2
  741.6 16.9 %copy-start.5 = (bf16[1,384,1024]{2,1,0:T(8,128)(2,1)S(1)}, bf16[1,384,1024]{2,1,0:T(8,128)(2,1)}, u32[]{:S(2)}) copy-start(bf16[1,384,1024]{2,1,0:T(8,128)(2,1)} %copy-done.4) | copy-start | bytes 2359300
  741.6 16.9 %copy-start.7 = (bf16[1,384,1024]{2,1,0:T(8,128)(2,1)S(1)}, bf16[1,384,1024]{2,1,0:T(8,128)(2,1)}, u32[]{:S(2)}) copy-start(bf16[1,384,1024]{2,1,0:T(8,128)(2,1)} %copy-done.6) | copy-start | bytes 2359300
Sparse Core Ops, SparseCore 0:
  280.8 154.9 all-gather.1
where the time goes:
time: 797 us; the launch traced here: 788 us
  blocking collectives  514 us (64%)
  local copies, waits for them, and re-layouts  158 us (20%)
  matrix products  62.2 us (8%)
  waiting for transfers between devices  33.3 us (4%)
  between operations  14 us (2%)
    all_to_all x1, blocking collectives, body(): lax.all_to_all(weighted, 'lat', split_axis=0, concat_axis=1, tiled=True)  112 us
    all_to_all x1, blocking collectives, body(): lax.all_to_all(mixed_coef, 'lat', split_axis=0, concat_axis=1, tiled=True)  110 us
    all_to_all x1, blocking collectives, body(): lax.all_to_all(synthesis, 'lat', split_axis=1, concat_axis=0, tiled=True)  109 us
    all_to_all x1, blocking collectives, body(): lax.all_to_all(coeffs, 'lat', split_axis=1, concat_axis=0, tiled=True)  108 us
    all_to_all x1, blocking collectives, body(): lax.all_to_all(mixing, 'chan', split_axis=3, concat_axis=2, tiled=True)  74.5 us
    all_gather x1, waiting for transfers between devices, body(): block_in = lax.all_gather(by_degree, 'chan', axis=2, tiled=True)  33.2 us
    reshape x2, local copies, waits for them, and re-layouts, body(): spread = gridded.reshape(M, rows_lat, 2, groups)  29.3 us
    unnamed x19, local copies, waits for them, and re-layouts  27.2 us
  transfers between devices with their start and end apart: 1, of which 1 were waited for; matrix products, arithmetic and copies ran while one was open for 6% of the time, Pallas kernels for 0%

commit v1 on v0

v1 whole, which is shorter than its diff:
```python
import functools
import math

import jax
import jax.numpy as jnp
from jax import lax
from jax.experimental import pallas as pl
from jax.sharding import PartitionSpec as P

M = 384
PIECES = (2, 1)


def fourier_table(number, length):
    orders = jnp.arange(number, dtype=jnp.int32)
    points = jnp.arange(length, dtype=jnp.int32)
    phases = orders[:, None] * points[None, :] % length
    angles = phases.astype(jnp.float32) * (2.0 * math.pi / length)
    factor = 1.0 / math.sqrt(length)
    return jnp.stack([jnp.cos(angles) * factor, -jnp.sin(angles) * factor]).astype(jnp.bfloat16)


def step_of(part):
    return next(count for count in (4, 3, 2, 1) if part % count == 0)


def price(legendre, columns):
    orders, degrees, points = legendre.shape
    return pl.CostEstimate(
        flops=2 * orders * degrees * points * columns,
        bytes_accessed=2 * orders * (degrees * points + (degrees + points) * columns),
        transcendentals=0,
    )


def analyse(legendre, gathered, chans):
    lats, orders, rows_lat, columns = gathered.shape
    degrees = legendre.shape[1] // lats
    part = orders // chans
    step = step_of(part)
    runs = part // step

    def kernel(table_ref, values_ref, out_ref):
        for at in range(step):
            values = values_ref[:, at].reshape(lats * rows_lat, columns)
            sums = jnp.dot(table_ref[at], values, preferred_element_type=jnp.float32)
            out_ref[:, 0, at] = sums.astype(jnp.bfloat16).reshape(lats, degrees, columns)

    return pl.pallas_call(
        kernel,
        grid=(orders // step,),
        in_specs=[
            pl.BlockSpec((step,) + legendre.shape[1:], lambda g: (g, 0, 0)),
            pl.BlockSpec((lats, step, rows_lat, columns), lambda g: (0, g, 0, 0)),
        ],
        out_specs=pl.BlockSpec(
            (lats, 1, step, degrees, columns), lambda g: (0, g // runs, g % runs, 0, 0)
        ),
        out_shape=jax.ShapeDtypeStruct((lats, chans, part, degrees, columns), jnp.bfloat16),
        cost_estimate=price(legendre, columns),
    )(legendre, gathered)


def synthesise(legendre, returned, rows_lat):
    lats, chans, part, degrees, columns = returned.shape
    orders = legendre.shape[0]
    step = step_of(part)
    runs = part // step

    def kernel(table_ref, values_ref, out_ref):
        for at in range(step):
            values = values_ref[:, 0, at].reshape(lats * degrees, columns)
            sums = lax.dot_general(
                table_ref[at],
                values,
                (((0,), (0,)), ((), ())),
                preferred_element_type=jnp.float32,
            )
            out_ref[:, at] = sums.astype(jnp.bfloat16).reshape(lats, rows_lat, columns)

    return pl.pallas_call(
        kernel,
        grid=(orders // step,),
        in_specs=[
            pl.BlockSpec((step,) + legendre.shape[1:], lambda g: (g, 0, 0)),
            pl.BlockSpec(
                (lats, 1, step, degrees, columns), lambda g: (0, g // runs, g % runs, 0, 0)
            ),
        ],
        out_specs=pl.BlockSpec((lats, step, rows_lat, columns), lambda g: (0, g, 0, 0)),
        out_shape=jax.ShapeDtypeStruct((lats, orders, rows_lat, columns), jnp.bfloat16),
        cost_estimate=price(legendre, columns),
    )(legendre, returned)


def body(chans, grid_in, quad_weights, legendre, mixing):
    groups = grid_in.shape[0]
    rows_lat = grid_in.shape[1]
    length = grid_in.shape[2]
    orders = legendre.shape[0]
    degrees = mixing.shape[1]
    lats = legendre.shape[1] // degrees
    part = -(-orders // chans)
    padding = part * chans - orders
    everyone = ("lat", "chan")

    channel = jnp.arange(chans * groups)
    place = channel // groups * (2 * groups) + channel % groups
    column = jnp.arange(2 * chans * groups)
    to_real = (column == place[:, None]).astype(jnp.bfloat16)
    to_imag = (column == place[:, None] + groups).astype(jnp.bfloat16)

    def spread_out(table):
        return jnp.einsum(
            "rlcd,rdy->lcy", mixing, table, preferred_element_type=jnp.float32
        ).astype(jnp.bfloat16)

    blocks = jnp.concatenate(
        [
            spread_out(jnp.stack([to_real, to_imag])),
            spread_out(jnp.stack([to_imag, -to_real])),
        ],
        axis=1,
    )
    weights = lax.all_gather(blocks, "chan", axis=0)
    fourier = fourier_table(M, length)
    spectra = jnp.einsum("ctn,rmn->mtrc", grid_in, fourier, preferred_element_type=jnp.float32)
    spectra = spectra * quad_weights[None, :, None, None]
    weighted = spectra.astype(jnp.bfloat16).reshape(M, rows_lat, 2 * groups)
    gathered = lax.all_to_all(weighted, "lat", split_axis=0, concat_axis=0, tiled=True)
    gathered = gathered.reshape(lats, orders, rows_lat, 2 * groups)
    fits = padding == 0 and rows_lat % 16 == 0 and degrees % 16 == 0
    if fits:
        outgoing = analyse(legendre, gathered, chans)
    else:
        whole = gathered.transpose(1, 0, 2, 3).reshape(orders, lats * rows_lat, 2 * groups)
        coeffs = jnp.einsum(
            "mlt,mtk->mlk", legendre, whole, preferred_element_type=jnp.float32
        ).astype(jnp.bfloat16)
        coeffs = jnp.pad(coeffs, ((0, padding), (0, 0), (0, 0)))
        outgoing = coeffs.reshape(chans, part, lats, degrees, 2 * groups)
        outgoing = outgoing.transpose(2, 0, 1, 3, 4)
    pieces = next(count for count in PIECES if part % count == 0)
    width = part // pieces
    place_lat = lax.axis_index("lat")
    peers = jnp.arange(lats).reshape(lats, 1, 1, 1, 1)

    def exchange(buffer, axes):
        flat = buffer.reshape((-1,) + buffer.shape[-3:])
        flat = lax.all_to_all(flat, axes, split_axis=0, concat_axis=0, tiled=True)
        return flat.reshape(buffer.shape)

    def mix(arrived):
        mixed = jnp.einsum(
            "ikmlx,klxy->limy", arrived, weights, preferred_element_type=jnp.float32
        ).astype(jnp.bfloat16)
        mixed = mixed.reshape(degrees, lats, width, chans, 2 * groups)
        return mixed.transpose(1, 3, 2, 0, 4)

    received = [exchange(outgoing[:, :, :width], ("lat", "chan"))]
    own = []
    for piece in range(1, pieces + 1):
        mixed = mix(received[-1])
        if piece < pieces:
            own.append(lax.dynamic_index_in_dim(mixed, place_lat, 0, keepdims=False))
            coming = outgoing[:, :, piece * width : (piece + 1) * width]
            mixed = jnp.where(peers >= place_lat, coming, mixed)
        received.append(exchange(mixed, ("lat", "chan")))
    if own:
        own = exchange(jnp.concatenate(own, axis=1), "chan")
    returned = []
    for piece in range(pieces):
        block = received[piece + 1]
        if piece < pieces - 1:
            mine = own[None, :, piece * width : (piece + 1) * width]
            block = jnp.where(peers == place_lat, mine, block)
        returned.append(jnp.where(peers >= place_lat, block, jnp.zeros_like(block)))
    returned = jnp.concatenate(returned, axis=2)
    if fits:
        synthesis = synthesise(legendre, returned, rows_lat)
    else:
        mixed_coef = returned.transpose(1, 2, 0, 3, 4)
        mixed_coef = mixed_coef.reshape(chans * part, lats * degrees, 2 * groups)[:orders]
        synthesis = jnp.einsum(
            "mlt,mlk->mtk", legendre, mixed_coef, preferred_element_type=jnp.float32
        ).astype(jnp.bfloat16)
        synthesis = synthesis.reshape(orders, lats, rows_lat, 2 * groups).transpose(1, 0, 2, 3)
    synthesis = synthesis.reshape(lats * orders, rows_lat, 2 * groups)
    gridded = lax.all_to_all(synthesis, "lat", split_axis=0, concat_axis=0, tiled=True)
    spread = gridded.reshape(M, rows_lat, 2, groups)
    restored = jnp.einsum("mtrc,rmn->ctn", spread, fourier, preferred_element_type=jnp.float32)
    return (restored + grid_in.astype(jnp.float32)).astype(jnp.bfloat16)


def solution(mesh):
    return jax.shard_map(
        functools.partial(body, mesh.shape["chan"]),
        mesh=mesh,
        in_specs=(
            P("chan", "lat", None),
            P("lat"),
            P("lat", None, None),
            P(None, "lat", "chan", None),
        ),
        out_specs=P("chan", "lat", None),
        check_vma=False,
    )
```

time: 797 us -> 553 us (0.69); the launches traced: 788 us -> 552 us
  blocking collectives: 514 us -> 220 us
  waiting for transfers between devices: 33.3 us -> 160 us
  local copies, waits for them, and re-layouts: 158 us -> 38.5 us
  Pallas kernels: 0 us -> 27.6 us
  starting transfers between devices: 0.01 us -> 15.7 us
  other arithmetic: 6.98 us -> 21.5 us
    all_to_all x5 -> x2, blocking collectives: 514 us -> 220 us  [the longest x1 111 us: body(): lax.all_to_all(weighted, 'lat', split_axis=0, concat_axis=0, tiled=True)]
    all_to_all x0 -> x4, waiting for transfers between devices: none -> 160 us  [exchange(): flat = lax.all_to_all(flat, axes, split_axis=0, concat_axis=0, tiled=True)]
    all_gather x1, waiting for transfers between devices: 33.2 us -> 0.01 us  [body(): weights = lax.all_gather(blocks, 'chan', axis=0)]
    reshape x2 -> x0, local copies, waits for them, and re-layouts: 29.3 us -> none  [body(): spread = gridded.reshape(M, rows_lat, 2, groups)]
    pallas_call x0 -> x2, Pallas kernels: none -> 27.6 us  [the longest x1 13.9 us: synthesise(): pl.pallas_call(kernel, grid=(orders // step,), in_specs=[pl.BlockSpec((st...]
    all_gather x1 -> x0, local copies, waits for them, and re-layouts: 25.8 us -> none  [body(): block_in = lax.all_gather(by_degree, 'chan', axis=2, tiled=True)]
    unnamed x19 -> x18, local copies, waits for them, and re-layouts: 27.2 us -> 3 us
    convert_element_type x3 -> x0, local copies, waits for them, and re-layouts: 20.9 us -> none  [the longest x1 6.97 us: body(): coeffs = jnp.einsum('mlt,mtk->mlk', legendre, lax.all_to_all(weighted, 'l...]
  transfers between devices with their start and end apart: 1 -> 5, of which waited for: 1 -> 3; matrix products, arithmetic and copies ran while one was open for 6% -> 10% of each run, Pallas kernels for 0% -> 2%
where the time goes in v1:
time: 553 us; the launch traced here: 552 us
  blocking collectives  220 us (40%)
  waiting for transfers between devices  160 us (29%)
  matrix products  55 us (10%)
  local copies, waits for them, and re-layouts  38.5 us (7%)
  Pallas kernels  27.6 us (5%)
  other arithmetic  21.5 us (4%)
  starting transfers between devices  15.7 us (3%)
  between operations  13.6 us (2%)
    all_to_all x4, waiting for transfers between devices, exchange(): flat = lax.all_to_all(flat, axes, split_axis=0, concat_axis=0, tiled=True)  160 us
    all_to_all x1, blocking collectives, body(): lax.all_to_all(weighted, 'lat', split_axis=0, concat_axis=0, tiled=True)  111 us
    all_to_all x1, blocking collectives, body(): lax.all_to_all(synthesis, 'lat', split_axis=0, concat_axis=0, tiled=True)  109 us
    dot_general x2, matrix products, mix(): jnp.einsum('ikmlx,klxy->limy', arrived, weights, preferred_element_type=j...  23.6 us
    all_to_all x4, starting transfers between devices, exchange(): flat = lax.all_to_all(flat, axes, split_axis=0, concat_axis=0, tiled=True)  15.7 us
    dot_general x1, matrix products, body(): jnp.einsum('mtrc,rmn->ctn', spread, fourier, preferred_element_type=jnp.f...  15.5 us
    pallas_call x1, Pallas kernels, synthesise(): pl.pallas_call(kernel, grid=(orders // step,), in_specs=[pl.BlockSpec((st...  13.9 us
    pallas_call x1, Pallas kernels, analyse(): pl.pallas_call(kernel, grid=(orders // step,), in_specs=[pl.BlockSpec((st...  13.7 us
  transfers between devices with their start and end apart: 5, of which 3 were waited for; matrix products, arithmetic and copies ran while one was open for 10% of the time, Pallas kernels for 2%

profile of v1, /device:TPU:0, one launch (start us, length us, event | category | flops | bytes accessed | tf_op | source)
XLA Modules:
  0.0 551.8 jit_solution(15293668838853564284)
XLA Ops:
  6.5 0.0 copy-start
  6.5 0.0 all-gather.3.cloned.1.call-start
  6.6 0.1 fusion.43
  6.7 0.2 fusion.41
  6.8 1.6 copy-done
  8.4 1.8 fusion.9
  10.2 1.8 fusion.10
  12.0 3.4 pad_maximum_fusion
  15.4 0.0 copy-start.8
  15.4 0.0 all-gather.3.cloned.1.call-update
  15.5 6.5 %multiply_convert_fusion.1 = (bf16[1,384,1024]{2,1,0:T(8,128)(2,1)S(1)}, bf16[1,384,1024]{2,1,0:T(8,128)(2,1)S(1)}) fusion(), kind=kLoop, calls=%fused_computation.35 | loop fusion | flops 7471104 | bytes 1572864 | tf_op jit(solution)/shard_map/convert.1
  21.9 0.0 copy-start.4
  21.9 0.0 copy-start.6
  21.9 0.0 copy-done.8
  21.9 12.3 %fusion.8 = bf16[384,48,2,64]{0,3,1,2:T(8,128)(2,1)S(1)} fusion(f32[48]{0:T(128)S(1)} %copy-done.8, bf16[64,48,1024]{2,1,0:T(8,128)(2,1)} %param.4, bf16[1,384,1024]{2,1,0:T(8,128)(2,1)S(1)} %get-tuple-element.7, bf16[1,384,1024]{2,1,0:T(8,128)(2,1)S(1)} %get-tuple-element.8), kind=kOutput, calls=%fused_computation.13 | convolution fusion | flops 4839702528 | bytes 12583104 | tf_op jit(solution)/shard_map/ctn,rmn->mtrc/dot_general | solution.py:127
  34.3 0.0 copy-done.4
  34.3 0.0 copy-done.6
  34.3 3.7 copy.59
  38.0 7.3 %copy.60 = bf16[384,48,128]{2,1,0:T(8,128)(2,1)} copy(bf16[384,48,128]{0,2,1:T(8,128)(2,1)} %bitcast.90) | data formatting | bytes 9437184 | tf_op jit(solution)/shard_map/reshape | solution.py:129
  45.2 111.1 %all_to_all.30 = bf16[384,48,128]{2,1,0:T(8,128)(2,1)} all-to-all(bf16[384,48,128]{2,1,0:T(8,128)(2,1)} %copy.60), channel_id=1, replica_groups=mesh['lat'=8,'chan'=4] {'lat'}, dimensions={0} | all-to-all | bytes 9437184 | tf_op jit(solution)/shard_map/all_to_all | solution.py:130
  156.3 13.7 %shard_map.46 = bf16[8,4,12,48,128]{4,3,2,1,0:T(8,128)(2,1)} custom-call(bf16[48,384,384]{2,1,0:T(8,128)(2,1)} %table_ref.3, bf16[8,48,48,128]{3,2,1,0:T(8,128)(2,1)} %bitcast.91), custom_call_target="tpu_custom_call" | custom-call | flops 1811939328 | bytes 23592960 | tf_op jit(solution)/shard_map/pallas_call | solution.py:49
  170.1 3.5 slice.8
  173.6 3.9 all-to-all-start.1
  177.4 54.3 %all-to-all-done.1 = bf16[32,6,48,128]{3,2,1,0:T(8,128)(2,1)S(1)} async-done(((bf16[32,6,48,128]{3,2,1,0:T(8,128)(2,1)}), bf16[32,6,48,128]{3,2,1,0:T(8,128)(2,1)S(1)}, u32[]{:S(2)}, u32[]{:S(2)}) %all-to-all-start.1) | async-done | bytes 2359328 | tf_op jit(solution)/shard_map/all_to_all | solution.py:150
  231.7 0.0 copy-start.3
  231.7 0.0 all-gather.3.cloned.1.call-done
  231.7 1.4 copy-done.3
  233.1 11.3 %fusion.13 = bf16[48,8,6,4,128]{4,1,3,2,0:T(8,128)(2,1)S(1)} fusion(bf16[4,48,128,512,1]{3,2,1,0,4:T(8,128)(2,1)} %bitcast.99, bf16[8,4,6,48,128]{4,3,2,1,0:T(8,128)(2,1)} %bitcast.98), kind=kOutput, calls=%fused_computation.22 | convolution fusion | flops 1209139200 | bytes 29884416 | tf_op jit(solution)/shard_map/ikmlx,klxy->limy/dot_general | solution.py:154
  244.4 0.0 copy-start.2
  244.4 6.6 %slice_select_fusion = bf16[8,4,6,48,128]{4,3,2,1,0:T(8,128)(2,1)} fusion(bf16[8,4,12,48,128]{4,3,2,1,0:T(8,128)(2,1)} %shard_map.46, bf16[48,8,6,4,128]{4,1,3,2,0:T(8,128)(2,1)S(1)} %fusion.13, pred[8]{0:T(512)(128)(4,1)S(1)} %iota_compare_fusion.3), kind=kLoop, calls=%fused_computation.24 | loop fusion | flops 1179648 | bytes 7077896 | tf_op jit(solution)/shard_map/jit(_where)/select_n | solution.py:167
  251.0 0.0 copy-done.2
  251.0 4.0 all-to-all-start.3
  255.0 2.3 dynamic-slice_bitcast_fusion
  257.3 0.8 copy.110
  258.2 51.3 %all-to-all-done.3 = bf16[32,6,48,128]{3,2,1,0:T(8,128)(2,1)S(1)} async-done(((bf16[32,6,48,128]{3,2,1,0:T(8,128)(2,1)}), bf16[32,6,48,128]{3,2,1,0:T(8,128)(2,1)S(1)}, u32[]{:S(2)}, u32[]{:S(2)}) %all-to-all-start.3) | async-done | bytes 2359328 | tf_op jit(solution)/shard_map/all_to_all | solution.py:150
  309.4 3.5 all-to-all-start.2
  312.9 12.3 %fusion.14 = bf16[8,4,6,48,128]{4,0,1,2,3:T(8,128)(2,1)} fusion(bf16[4,48,128,512,1]{3,2,1,0,4:T(8,128)(2,1)} %bitcast.100, bf16[8,4,6,48,128]{4,3,2,1,0:T(8,128)(2,1)S(1)} %bitcast.93), kind=kOutput, calls=%fused_computation.23 | convolution fusion | flops 1209139200 | bytes 29884416 | tf_op jit(solution)/shard_map/ikmlx,klxy->limy/dot_general | solution.py:154
  325.2 4.6 copy.69
  329.8 0.0 all-to-all-done.2
  329.8 4.4 all-to-all-start.4
  334.3 54.3 %all-to-all-done.4 = bf16[32,6,48,128]{3,2,1,0:T(8,128)(2,1)} async-done(((bf16[32,6,48,128]{3,2,1,0:T(8,128)(2,1)}), bf16[32,6,48,128]{3,2,1,0:T(8,128)(2,1)}, u32[]{:S(2)}, u32[]{:S(2)}) %all-to-all-start.4) | async-done | bytes 2359328 | tf_op jit(solution)/shard_map/all_to_all | solution.py:150
  388.6 2.1 select_select_fusion
  390.7 2.6 pad_maximum_fusion.1.values_ref
  393.3 13.9 %shard_map.47 = bf16[8,48,48,128]{3,2,1,0:T(8,128)(2,1)} custom-call(bf16[48,384,384]{2,1,0:T(8,128)(2,1)} %table_ref.3, bf16[8,4,12,48,128]{4,3,2,1,0:T(8,128)(2,1)} %pad_maximum_fusion.1.values_ref), custom_call_target="tpu_custom_call" | custom-call | flops 1811939328 | bytes 23592960 | tf_op jit(solution)/shard_map/pallas_call | solution.py:81
  407.2 108.9 %all_to_all.31 = bf16[384,48,128]{2,1,0:T(8,128)(2,1)} all-to-all(bf16[384,48,128]{2,1,0:T(8,128)(2,1)} %bitcast.92), channel_id=1, replica_groups=mesh['lat'=8,'chan'=4] {'lat'}, dimensions={0} | all-to-all | bytes 9437184 | tf_op jit(solution)/shard_map/all_to_all | solution.py:189
  516.1 0.0 copy-start.5
  516.1 0.0 copy-start.7
  516.1 7.1 %copy.70 = bf16[384,48,128]{0,2,1:T(8,128)(2,1)} copy(bf16[384,48,128]{2,1,0:T(8,128)(2,1)} %all_to_all.31) | data formatting | bytes 9437184 | tf_op jit(solution)/shard_map/all_to_all | solution.py:189
  523.2 0.0 copy-done.5
  523.2 0.0 copy-done.7
  523.2 15.5 %fusion.4 = bf16[64,48,1024]{2,0,1:T(8,128)(2,1)S(1)} fusion(bf16[64,48,1024]{2,1,0:T(8,128)(2,1)} %param.4, bf16[384,48,2,64]{0,3,2,1:T(8,128)(2,1)} %bitcast.97, bf16[1,384,1024]{2,1,0:T(8,128)(2,1)S(1)} %copy-done.5, bf16[1,384,1024]{2,1,0:T(8,128)(2,1)S(1)} %copy-done.7), kind=kOutput, calls=%fused_computation.5 | convolution fusion | flops 4844421120 | bytes 18874368 | tf_op jit(solution)/shard_map/mtrc,rmn->ctn/dot_general | solution.py:191
  538.7 0.0 copy-start.1
  538.7 6.2 %copy.72 = bf16[64,48,1024]{2,1,0:T(8,128)(2,1)} copy(bf16[64,48,1024]{2,0,1:T(8,128)(2,1)S(1)} %fusion.4) | data formatting | bytes 12582912 | tf_op jit(solution)/shard_map/convert_element_type | solution.py:192
  545.0 0.0 copy-done.1
  (4 shorter events, 0.0 us)
Async XLA Ops:
  6.5 1.9 copy-start
  6.5 225.2 %all-gather.3.cloned.1.call-start = ((), (), s32[]{:S(2)}) async-start(), calls=%async_computation.6 | async-start | bytes 31457280 | tf_op jit(solution)/shard_map/all_gather | solution.py:125
  15.4 6.5 %copy-start.8 = (f32[48]{0:T(128)S(1)}, f32[48]{0:T(128)}, u32[]{:S(2)}) copy-start(f32[48]{0:T(128)} %param.5) | copy-start | bytes 580
  21.9 12.4 %copy-start.4 = (bf16[1,384,1024]{2,1,0:T(8,128)(2,1)}, bf16[1,384,1024]{2,1,0:T(8,128)(2,1)S(1)}, u32[]{:S(2)}) copy-start(bf16[1,384,1024]{2,1,0:T(8,128)(2,1)S(1)} %get-tuple-element.7) | copy-start | bytes 2359300
  21.9 12.4 %copy-start.6 = (bf16[1,384,1024]{2,1,0:T(8,128)(2,1)}, bf16[1,384,1024]{2,1,0:T(8,128)(2,1)S(1)}, u32[]{:S(2)}) copy-start(bf16[1,384,1024]{2,1,0:T(8,128)(2,1)S(1)} %get-tuple-element.8) | copy-start | bytes 2359300
  173.6 58.2 %all-to-all-start.1 = ((bf16[32,6,48,128]{3,2,1,0:T(8,128)(2,1)}), bf16[32,6,48,128]{3,2,1,0:T(8,128)(2,1)S(1)}, u32[]{:S(2)}, u32[]{:S(2)}) async-start(bf16[32,6,48,128]{3,2,1,0:T(8,128)(2,1)} %bitcast.6), calls=%async_computation.1 | async-start | bytes 4718592 | tf_op jit(solution)/shard_map/all_to_all | solution.py:150
  231.7 1.4 copy-start.3
  244.4 6.6 %copy-start.2 = (bf16[48,8,6,4,128]{4,1,3,2,0:T(8,128)(2,1)}, bf16[48,8,6,4,128]{4,1,3,2,0:T(8,128)(2,1)S(1)}, u32[]{:S(2)}) copy-start(bf16[48,8,6,4,128]{4,1,3,2,0:T(8,128)(2,1)S(1)} %fusion.13) | copy-start | bytes 7077892
  251.0 58.4 %all-to-all-start.3 = ((bf16[32,6,48,128]{3,2,1,0:T(8,128)(2,1)}), bf16[32,6,48,128]{3,2,1,0:T(8,128)(2,1)S(1)}, u32[]{:S(2)}, u32[]{:S(2)}) async-start(bf16[32,6,48,128]{3,2,1,0:T(8,128)(2,1)} %bitcast.95), calls=%async_computation.3 | async-start | bytes 4718592 | tf_op jit(solution)/shard_map/all_to_all | solution.py:150
  309.4 20.4 %all-to-all-start.2 = ((bf16[4,6,48,128]{3,2,1,0:T(8,128)(2,1)}), bf16[4,6,48,128]{3,2,1,0:T(8,128)(2,1)S(1)}, u32[]{:S(2)}, u32[]{:S(2)}) async-start(bf16[4,6,48,128]{3,2,1,0:T(8,128)(2,1)} %bitcast.89), calls=%async_computation.2 | async-start | bytes 589824 | tf_op jit(solution)/shard_map/all_to_all | solution.py:150
  329.8 58.7 %all-to-all-start.4 = ((bf16[32,6,48,128]{3,2,1,0:T(8,128)(2,1)}), bf16[32,6,48,128]{3,2,1,0:T(8,128)(2,1)}, u32[]{:S(2)}, u32[]{:S(2)}) async-start(bf16[32,6,48,128]{3,2,1,0:T(8,128)(2,1)} %bitcast.96), calls=%async_computation.4 | async-start | bytes 4718592 | tf_op jit(solution)/shard_map/all_to_all | solution.py:150
  516.1 7.1 %copy-start.5 = (bf16[1,384,1024]{2,1,0:T(8,128)(2,1)S(1)}, bf16[1,384,1024]{2,1,0:T(8,128)(2,1)}, u32[]{:S(2)}) copy-start(bf16[1,384,1024]{2,1,0:T(8,128)(2,1)} %copy-done.4) | copy-start | bytes 2359300
  516.1 7.1 %copy-start.7 = (bf16[1,384,1024]{2,1,0:T(8,128)(2,1)S(1)}, bf16[1,384,1024]{2,1,0:T(8,128)(2,1)}, u32[]{:S(2)}) copy-start(bf16[1,384,1024]{2,1,0:T(8,128)(2,1)} %copy-done.6) | copy-start | bytes 2359300
  538.7 6.3 %copy-start.1 = (bf16[2,48,64,256]{3,2,1,0:T(8,128)(2,1)S(1)}, bf16[2,48,64,256]{3,2,1,0:T(8,128)(2,1)}, u32[]{:S(2)}) copy-start(bf16[2,48,64,256]{3,2,1,0:T(8,128)(2,1)} %param.7) | copy-start | bytes 9437188
Sparse Core Ops, SparseCore 0:
  15.6 157.4 all-gather.2
